TPU v7x, 32 devices: a whole 2x2x4 slice. The times are simulated.
32 devices in a mesh: rows: 8 (over z, y), cols: 4 (over x, core).
Axes of the slice: x: 2, y: 2, z: 4, core: 2. Of those that a mesh axis runs over, the one named last changes fastest.
Arguments:
- blocks: bfloat16 [32, 4, 3, 128, 128], P('rows', 'cols'), may hold values from -1.1953125 to 1.1953125
- block_cols: int32 [32, 4, 3], P('rows', 'cols'), may hold values from 0 to 31, as said below
Outputs:
- square_blocks: bfloat16 [32, 4, 36, 128, 128], P('rows', 'cols')
- square_cols: int32 [32, 4, 36], P('rows', 'cols')
- square_start: int32 [32, 4], P('rows', 'cols')
Inputs may be any that keep to these rules, and one draw needn't show every extreme that they name: Block-row i lies in panel p = i // 4; every block_cols[i, g, s] is a block-column congruent to g modulo 4 among block-rows 4 * (p - 4) to 4 * (p + 4) - 1, taken modulo 32; the three entries of one group differ; the block-columns i - 1, i and i + 1 (modulo 32) are always among a row's entries.
All inputs are finite; a program needn't handle non-finite values.
Results may differ from a plain program's by a relative error of at most 0.001.
Values may be sent and summed in bfloat16 or wider, within the bound.
A program may use at most 64 MiB of HBM per device.

v0:
```python
import functools

import jax
import jax.numpy as jnp
from jax import lax
from jax.experimental import pallas as pl
from jax.experimental.pallas import tpu as pltpu
from jax.sharding import PartitionSpec as P

HP = 4


def shifted(block, axis, distance):
    devices = range(lax.axis_size(axis))
    route = [((i - distance) % len(devices), i) for i in devices]
    return lax.ppermute(block, axis, route)


def unique_slots(candidates):
    width = candidates.shape[-1]
    ordered = jnp.sort(candidates, axis=-1)
    firsts = jnp.concatenate(
        [jnp.ones(ordered.shape[:-1] + (1,), dtype=bool), ordered[..., 1:] != ordered[..., :-1]],
        axis=-1,
    )
    marks = firsts.astype(jnp.int32)
    totals = jnp.sum(marks, axis=-1)
    ranking = jnp.sum(
        marks[..., None, :] * (ordered[..., None, :] < candidates[..., :, None]).astype(jnp.int32),
        axis=-1,
    )
    places = jnp.cumsum(marks, axis=-1) - 1
    slot_ids = jnp.arange(width, dtype=jnp.int32)
    chosen = (places[..., None, :] == slot_ids[:, None]) & firsts[..., None, :]
    columns = jnp.sum(jnp.where(chosen, ordered[..., None, :], 0), axis=-1).astype(jnp.int32)
    columns = jnp.where(slot_ids < totals[..., None], columns, -1)
    onehot = (ranking[..., None, :] == slot_ids[:, None]).astype(jnp.float32)
    return (columns, onehot, totals)


def on_device(blocks, block_cols):
    panel_rows = block_cols.shape[0]
    per_group = block_cols.shape[2]
    block_size = blocks.shape[-1]
    cycle_size = lax.axis_size("rows")
    block_rows = panel_rows * cycle_size
    panel_id = lax.axis_index("rows")
    left_vals, left_cols = (
        lax.all_gather(blocks, "cols", axis=1, tiled=True),
        lax.all_gather(block_cols, "cols", axis=1, tiled=True),
    )
    groups = left_cols.shape[1]
    row_slots = groups * per_group
    left_vals = left_vals.reshape(panel_rows, row_slots, block_size, block_size)
    left_cols = left_cols.reshape(panel_rows, row_slots)
    own_panel = (blocks[:, 0], block_cols[:, 0])
    pieces = []
    for offset in range(-HP, HP):
        if offset == 0:
            pieces.append(own_panel)
        else:
            pieces.append(shifted((own_panel[0], own_panel[1]), "rows", -offset))
    win_vals = jnp.concatenate([piece[0] for piece in pieces], axis=0)
    win_cols = jnp.concatenate([piece[1] for piece in pieces], axis=0)
    window_base = (panel_id - HP) * panel_rows % block_rows
    local_index = ((left_cols - window_base) % block_rows).astype(jnp.int32)
    right_vals = win_vals[local_index]
    right_cols = win_cols[local_index]
    products = jnp.einsum(
        "ptab,ptsbc->ptsac", left_vals, right_vals, preferred_element_type=jnp.float32
    )
    candidates = right_cols.reshape(panel_rows, row_slots * per_group)
    columns, onehot, totals = unique_slots(candidates)
    merged = jnp.einsum(
        "poq,pqac->poac",
        onehot,
        products.reshape(panel_rows, row_slots * per_group, block_size, block_size),
        precision=lax.Precision.HIGHEST,
    )
    merged_blocks = merged.astype(jnp.bfloat16)
    panel_total = jnp.sum(totals)
    all_totals = lax.all_gather(panel_total.reshape(1), "rows", axis=0, tiled=True)
    earlier = jnp.sum(jnp.where(jnp.arange(cycle_size, dtype=jnp.int32) < panel_id, all_totals, 0))
    starts = earlier + jnp.cumsum(totals) - totals
    return (merged_blocks[:, None], columns[:, None], starts[:, None])


NY = 2
SPANS = (2, 5, 5)
STAGES = (1, 2, 3, 3)
CROSS = 1
VMEM_LIMIT = 16 * 1024 * 1024


def popcount(x, width):
    total = x & 1
    for b in range(1, width):
        total = total + ((x >> b) & 1)
    return total


def gather_kernel(
    sizes, own_ref, own_cols_ref, win_ref, left_ref, meta_ref,
    cols_buf, cols_smem, mask_smem,
    recv_sem, send_sem, crecv_sem, csend_sem, prow_recv, prow_send,
    lrecv_sem, lsend_sem, local_sem,
):
    R, C, PB, KG = sizes
    Z = R // NY
    CHUNKS = len(SPANS)
    begins = [sum(SPANS[:q]) for q in range(CHUNKS)]
    r = lax.axis_index("rows")
    c = lax.axis_index("cols")
    z, y = r // NY, r % NY
    other_y = 1 - y
    core_peer = (c // 2) * 2 + (1 - c % 2)
    x_peer = (c + 2) % C
    y_row = z * NY + other_y
    up_row, down_row = (z + 1) * NY + y, (z - 1) * NY + y
    has_up, has_down = z < Z - 1, z > 0
    UP, DOWN, SIDE = 0, 1, 2
    targets = {UP: up_row, DOWN: down_row, SIDE: y_row}

    local = [
        pltpu.make_async_copy(own_ref, win_ref.at[r], local_sem.at[0]),
        pltpu.make_async_copy(own_ref, left_ref.at[c], local_sem.at[1]),
        pltpu.make_async_copy(own_cols_ref, cols_buf.at[r, c], local_sem.at[2]),
    ]

    barrier = pltpu.get_barrier_semaphore()
    for cp in local:
        cp.start()

    def greet(rr, cc):
        pl.semaphore_signal(barrier, inc=1, device_id=(rr, cc), device_id_type=pl.DeviceIdType.MESH)

    greet(y_row, c)
    for d in range(1, C):
        greet(r, (c + d) % C)
    pl.when(has_up)(lambda: greet(up_row, c))
    pl.when(has_down)(lambda: greet(down_row, c))
    pl.semaphore_wait(barrier, C + jnp.minimum(z, 1) + jnp.minimum(Z - 1 - z, 1))

    def part(ref, row, chunk):
        return ref.at[row, pl.ds(begins[chunk], SPANS[chunk])]

    def chunk_copy(way, row, chunk):
        src = part(win_ref, row, chunk)
        return pltpu.make_async_remote_copy(
            src_ref=src, dst_ref=part(win_ref, row, chunk),
            send_sem=send_sem.at[way, row, chunk], recv_sem=recv_sem.at[row, chunk],
            device_id=(targets[way], c), device_id_type=pl.DeviceIdType.MESH,
        )

    def prow_copy(way, row):
        return pltpu.make_async_remote_copy(
            src_ref=cols_buf.at[row], dst_ref=cols_buf.at[row],
            send_sem=prow_send.at[way, row], recv_sem=prow_recv.at[row],
            device_id=(targets[way], c), device_id_type=pl.DeviceIdType.MESH,
        )

    def cols_copy(cc, group, d):
        return pltpu.make_async_remote_copy(
            src_ref=cols_buf.at[r, group], dst_ref=cols_buf.at[r, group],
            send_sem=csend_sem.at[d], recv_sem=crecv_sem.at[group],
            device_id=(r, cc), device_id_type=pl.DeviceIdType.MESH,
        )

    def left_copy(cc, group, d):
        return pltpu.make_async_remote_copy(
            src_ref=left_ref.at[group], dst_ref=left_ref.at[group],
            send_sem=lsend_sem.at[d], recv_sem=lrecv_sem.at[group],
            device_id=(r, cc), device_id_type=pl.DeviceIdType.MESH,
        )

    def both(act):
        pl.when(has_up)(lambda: act(UP))
        pl.when(has_down)(lambda: act(DOWN))

    def send_own(chunks):
        def act(way):
            for q in chunks:
                chunk_copy(way, r, q).start()
        both(act)

    local[2].wait()
    for d in range(1, C):
        cols_copy((c + d) % C, c, d).start()
    local[0].wait()
    cross = list(range(CROSS))
    rest = list(range(CROSS, CHUNKS))
    stages = STAGES + (CHUNKS,)
    along, aside = rest + cross, cross + rest

    def send_side(chunks):
        for q in chunks:
            chunk_copy(SIDE, r, q).start()

    send_side(cross)
    send_own(along[: stages[0]])
    send_side(aside[CROSS : stages[0]])
    for d in range(1, C):
        cols_copy(c, (c + d) % C, d).wait_recv()

    both(lambda way: prow_copy(way, r).start())
    prow_copy(SIDE, r).start()
    send_own(along[stages[0] : stages[1]])
    send_side(aside[max(CROSS, stages[0]) : stages[1]])
    local[1].wait()
    left_copy(x_peer, c, 0).start()
    left_copy(core_peer, c, 1).start()

    def from_planes(d, act):
        @pl.when(z >= d)
        def _():
            act(z - d, UP, has_up)

        @pl.when(z + d < Z)
        def _():
            act(z + d, DOWN, has_down)

    def pass_prow(plane, way, more):
        row = plane * NY + y
        prow_copy(way, row).wait_recv()
        pl.when(more)(lambda: prow_copy(way, row).start())
        prow_copy(SIDE, row).start()

    for d in range(1, Z):
        from_planes(d, pass_prow)
        last = CHUNKS if d == Z - 1 else stages[d + 1]
        send_own(along[stages[d] : last])
        send_side(aside[max(CROSS, stages[d]) : last])
    for q in cross:
        chunk_copy(SIDE, y_row, q).wait_recv()
        both(lambda way: chunk_copy(way, y_row, q).start())

    def pass_chunk(q, side):
        def act(plane, way, more):
            row = plane * NY + (y if side else other_y)
            chunk_copy(way, row, q).wait_recv()
            pl.when(more)(lambda: chunk_copy(way, row, q).start())
            if side and q >= CROSS:
                chunk_copy(SIDE, row, q).start()
        return act

    def pass_plane(d):
        for q in along:
            from_planes(d, pass_chunk(q, True))
        for q in cross:
            from_planes(d, pass_chunk(q, False))

    pass_plane(1)

    left_copy(c, x_peer, 0).wait_recv()
    left_copy(core_peer, x_peer, 2).start()

    def each_plane(act):
        for d in range(1, Z):
            from_planes(d, lambda plane, way, more: act(plane))

    prow_copy(SIDE, y_row).wait_recv()
    each_plane(lambda plane: prow_copy(SIDE, plane * NY + other_y).wait_recv())
    to_smem = pltpu.make_async_copy(cols_buf, cols_smem, local_sem.at[3])
    to_smem.start()
    to_smem.wait()

    def fill_mask(rr, carry):
        for i in range(PB):
            m = jnp.int32(0)
            for s in range(KG):
                m = m | (jnp.int32(1) << (cols_smem[rr, c, s, 0, i] // C))
            mask_smem[rr * PB + i] = m
        return carry

    lax.fori_loop(0, R, fill_mask, jnp.int32(0))
    classes = R * PB // C

    def row_mask(rr, i):
        m = jnp.int32(0)
        for g in range(C):
            for s in range(KG):
                m = m | mask_smem[cols_smem[rr, g, s, 0, i]]
        return m

    def count_panel(rr, total):
        for i in range(PB):
            total = total + popcount(row_mask(rr, i), classes)
        return total

    start = lax.fori_loop(0, r, count_panel, jnp.int32(0))
    base = PB * C * KG * KG
    for i in range(PB):
        m = row_mask(r, i)
        meta_ref[base + PB * C * KG + i] = m
        meta_ref[base + PB * C * KG + PB + i] = start
        ranks = jnp.int32(0)
        rank = jnp.int32(0)
        for a in range(classes):
            ranks = ranks | (rank << (4 * a))
            rank = rank + ((m >> a) & 1)
        start = start + rank
        for g in range(C):
            for s in range(KG):
                e = g * KG + s
                k = cols_smem[r, g, s, 0, i]
                meta_ref[base + i * C * KG + e] = k
                for t in range(KG):
                    a = cols_smem[k // PB, c, t, 0, k % PB] // C
                    meta_ref[(i * C * KG + e) * KG + t] = (ranks >> (4 * a)) & 15

    for d in range(2, Z):
        pass_plane(d)
    for q in rest:
        chunk_copy(SIDE, y_row, q).wait_recv()
        each_plane(lambda plane: chunk_copy(SIDE, plane * NY + other_y, q).wait_recv())
    left_copy(c, core_peer, 1).wait_recv()
    left_copy(c, (core_peer + 2) % C, 2).wait_recv()

    for d in range(1, C):
        cols_copy((c + d) % C, c, d).wait_send()
    left_copy(x_peer, c, 0).wait_send()
    left_copy(core_peer, c, 1).wait_send()
    left_copy(core_peer, x_peer, 2).wait_send()
    for q in range(CHUNKS):
        chunk_copy(SIDE, r, q).wait_send()
        both(lambda way: chunk_copy(way, r, q).wait_send())
        if q in cross:
            both(lambda way: chunk_copy(way, y_row, q).wait_send())
    both(lambda way: prow_copy(way, r).wait_send())
    prow_copy(SIDE, r).wait_send()

    def sent(plane, way, more):
        row = plane * NY + y
        prow_copy(SIDE, row).wait_send()
        for q in rest:
            chunk_copy(SIDE, row, q).wait_send()

        @pl.when(more)
        def _():
            prow_copy(way, row).wait_send()
            for q in range(CHUNKS):
                chunk_copy(way, row, q).wait_send()
            for q in cross:
                chunk_copy(way, plane * NY + other_y, q).wait_send()

    for d in range(1, Z):
        from_planes(d, sent)


def square_kernel(
    sizes, meta_ref, left_ref, win_ref, out_ref, cols_ref, start_ref,
    acc, zeros, rows, cols_smem, start_smem, row_sem, fill_sem, small_sem,
):
    R, C, PB, KG = sizes
    me = lax.axis_index("cols")
    slots = C * KG * KG
    classes = R * PB // C
    base = PB * slots
    zeros[...] = jnp.zeros_like(zeros)

    def fill(i):
        return pltpu.make_async_copy(
            zeros, out_ref.at[i, 0, pl.ds(classes, slots - classes)], fill_sem.at[i]
        )

    def store(i):
        return pltpu.make_async_copy(
            rows.at[i], out_ref.at[i, 0, pl.ds(0, classes)], row_sem.at[i]
        )

    for i in range(PB):
        fill(i).start()
    for i in range(PB):
        m = meta_ref[base + PB * C * KG + i]
        start_smem[0, i] = meta_ref[base + PB * C * KG + PB + i]
        for o in range(slots):
            cols_smem[i, 0, o] = -1
        rank = jnp.int32(0)
        for a in range(classes):
            bit = (m >> a) & 1
            cols_smem[i, 0, rank] = jnp.where(bit == 1, a * C + me, -1)
            rank = rank + bit
    small = [
        pltpu.make_async_copy(cols_smem, cols_ref, small_sem.at[0]),
        pltpu.make_async_copy(start_smem, start_ref, small_sem.at[1]),
    ]
    for cp in small:
        cp.start()
    for i in range(PB):
        acc[...] = jnp.zeros_like(acc)
        for g in range(C):
            for s in range(KG):
                e = g * KG + s
                k = meta_ref[base + i * C * KG + e]
                lhs = left_ref[g, i * KG + s]
                for t in range(KG):
                    o = meta_ref[(i * C * KG + e) * KG + t]
                    acc[o] += jnp.dot(lhs, win_ref[k, t], preferred_element_type=jnp.float32)
        for o in range(classes):
            rows[i, o] = acc[o].astype(rows.dtype)
        store(i).start()
    for cp in small:
        cp.wait()
    for i in range(PB):
        fill(i).wait()
        store(i).wait()


def fast_on_device(blocks, block_cols):
    R, C = lax.axis_size("rows"), lax.axis_size("cols")
    PB, KG, BS = block_cols.shape[0], block_cols.shape[2], blocks.shape[-1]
    sizes = (R, C, PB, KG)
    slots = C * KG * KG
    vm = pl.BlockSpec(memory_space=pltpu.VMEM)
    hbm = pl.BlockSpec(memory_space=pltpu.HBM)
    sm = pl.BlockSpec(memory_space=pltpu.SMEM)
    dma = pltpu.SemaphoreType.DMA
    win, left, meta = pl.pallas_call(
        functools.partial(gather_kernel, sizes),
        out_shape=(
            jax.ShapeDtypeStruct((R, PB * KG, BS, BS), blocks.dtype),
            jax.ShapeDtypeStruct((C, PB * KG, BS, BS), blocks.dtype),
            jax.ShapeDtypeStruct((PB * slots + PB * C * KG + 2 * PB,), jnp.int32),
        ),
        in_specs=[hbm, hbm],
        out_specs=(vm, vm, sm),
        scratch_shapes=[
            pltpu.VMEM((R, C, KG, 1, PB), jnp.int32),
            pltpu.SMEM((R, C, KG, 1, PB), jnp.int32),
            pltpu.SMEM((R * PB,), jnp.int32),
            dma((R, len(SPANS))), dma((3, R, len(SPANS))), dma((C,)), dma((C,)),
            dma((R,)), dma((3, R)), dma((C,)), dma((3,)), dma((4,)),
        ],
        compiler_params=pltpu.CompilerParams(
            collective_id=0, has_side_effects=True, vmem_limit_bytes=VMEM_LIMIT
        ),
    )(
        pltpu.with_memory_space_constraint(blocks.reshape(PB * KG, BS, BS), pltpu.HBM),
        pltpu.with_memory_space_constraint(jnp.transpose(block_cols, (2, 1, 0)), pltpu.HBM),
    )
    out, cols, start = pl.pallas_call(
        functools.partial(square_kernel, sizes),
        out_shape=(
            pltpu.HBM((PB, 1, slots, BS, BS), blocks.dtype),
            pltpu.HBM((PB, 1, slots), jnp.int32),
            pltpu.HBM((1, PB), jnp.int32),
        ),
        in_specs=[sm, vm, vm],
        out_specs=(hbm, hbm, hbm),
        scratch_shapes=[
            pltpu.VMEM((R * PB // C, BS, BS), jnp.float32),
            pltpu.VMEM((slots - R * PB // C, BS, BS), blocks.dtype),
            pltpu.VMEM((PB, R * PB // C, BS, BS), blocks.dtype),
            pltpu.SMEM((PB, 1, slots), jnp.int32),
            pltpu.SMEM((1, PB), jnp.int32),
            dma((PB,)), dma((PB,)), dma((2,)),
        ],
        compiler_params=pltpu.CompilerParams(vmem_limit_bytes=VMEM_LIMIT),
    )(meta, left, win.reshape(R * PB, KG, BS, BS))
    return out, cols, start.T


def solution(mesh):
    in_specs = (P("rows", "cols", None, None, None), P("rows", "cols", None))
    out_specs = (P("rows", "cols", None, None, None), P("rows", "cols", None), P("rows", "cols"))
    body = fast_on_device if mesh.shape["rows"] == 2 * HP else on_device
    return jax.shard_map(
        body, mesh=mesh, in_specs=in_specs, out_specs=out_specs, check_vma=False
    )
```

profile of v0, /device:TPU:0, one launch (start us, length us, event | category | flops | bytes accessed | tf_op | source)
XLA Modules:
  0.0 46.0 jit_solution(14081231825633658632)
XLA Ops:
  0.6 41.5 %shard_map.49 = (bf16[8,12,128,128]{3,2,1,0:T(8,128)(2,1)S(1)}, bf16[4,12,128,128]{3,2,1,0:T(8,128)(2,1)S(1)}, s32[200]{0:T(256)S(1)}) custom-call(bf16[12,128,128]{2,1,0:T(8,128)(2,1)} %bitcast.5, s32[3,1,4]{2,1,0:T(1,128)} %bitcast.6), custom_call_target="tpu_custom_call" | custom-call | tf_op jit(solution)/shard_map/pallas_call | solution.py:418
  42.2 3.8 %shard_map.50 = (bf16[4,1,36,128,128]{4,3,2,1,0:T(8,128)(2,1)}, s32[4,1,36]{2,1,0:T(1,128)}, s32[1,4]{1,0:T(1,128)}) custom-call(s32[200]{0:T(256)S(1)} %get-tuple-element.9.meta_ref, bf16[4,12,128,128]{3,2,1,0:T(8,128)(2,1)S(1)} %get-tuple-element.10.left_ref, bf16[32,3,128,128]{3,2,1,0:T(8,128)(2,1)S(1)} %bitcast.4), custom_call_target="tpu_custom_call" | custom-call | tf_op jit(solution)/shard_map/pallas_call | solution.py:441
where the time goes:
time: 46.1 us; the launch traced here: 46 us
  Pallas kernels  45.3 us (98%)
  between operations  0.64 us (1%)
    pallas_call x1, Pallas kernels, fast_on_device(): pl.pallas_call(functools.partial(gather_kernel, sizes), out_shape=(jax.Sh...  41.5 us
    pallas_call x1, Pallas kernels, fast_on_device(): pl.pallas_call(functools.partial(square_kernel, sizes), out_shape=(pltpu....  3.79 us

commit v1 on v0

--- a/solution.py
+++ b/solution.py
@@ -87,7 +87,7 @@
 
 NY = 2
 SPANS = (2, 5, 5)
-STAGES = (1, 2, 3, 3)
+FILL = 1
 CROSS = 1
 VMEM_LIMIT = 16 * 1024 * 1024
 
@@ -189,23 +189,21 @@
     local[0].wait()
     cross = list(range(CROSS))
     rest = list(range(CROSS, CHUNKS))
-    stages = STAGES + (CHUNKS,)
-    along, aside = rest + cross, cross + rest
 
     def send_side(chunks):
         for q in chunks:
             chunk_copy(SIDE, r, q).start()
 
     send_side(cross)
-    send_own(along[: stages[0]])
-    send_side(aside[CROSS : stages[0]])
+    send_own(rest[:1])
+    send_side(rest[:1])
     for d in range(1, C):
         cols_copy(c, (c + d) % C, d).wait_recv()
 
     both(lambda way: prow_copy(way, r).start())
     prow_copy(SIDE, r).start()
-    send_own(along[stages[0] : stages[1]])
-    send_side(aside[max(CROSS, stages[0]) : stages[1]])
+    send_own(rest[1:])
+    send_side(rest[1:])
     local[1].wait()
     left_copy(x_peer, c, 0).start()
     left_copy(core_peer, c, 1).start()
@@ -225,34 +223,49 @@
         pl.when(more)(lambda: prow_copy(way, row).start())
         prow_copy(SIDE, row).start()
 
-    for d in range(1, Z):
-        from_planes(d, pass_prow)
-        last = CHUNKS if d == Z - 1 else stages[d + 1]
-        send_own(along[stages[d] : last])
-        send_side(aside[max(CROSS, stages[d]) : last])
-    for q in cross:
-        chunk_copy(SIDE, y_row, q).wait_recv()
-        both(lambda way: chunk_copy(way, y_row, q).start())
-
-    def pass_chunk(q, side):
+    def pass_chunk(q):
         def act(plane, way, more):
-            row = plane * NY + (y if side else other_y)
+            row = plane * NY + y
             chunk_copy(way, row, q).wait_recv()
             pl.when(more)(lambda: chunk_copy(way, row, q).start())
-            if side and q >= CROSS:
-                chunk_copy(SIDE, row, q).start()
+            chunk_copy(SIDE, row, q).start()
         return act
 
-    def pass_plane(d):
-        for q in along:
-            from_planes(d, pass_chunk(q, True))
-        for q in cross:
-            from_planes(d, pass_chunk(q, False))
-
-    pass_plane(1)
-
-    left_copy(c, x_peer, 0).wait_recv()
-    left_copy(core_peer, x_peer, 2).start()
+    def pass_cross(q, line):
+        def act(plane, way, more):
+            @pl.when(more)
+            def _():
+                chunk_copy(way, plane * NY + line, q).wait_recv()
+                chunk_copy(way, plane * NY + line, q).start()
+        return act
+
+    def take_cross(q, line):
+        def act(plane, way, more):
+            pl.when(jnp.logical_not(more))(
+                lambda: chunk_copy(way, plane * NY + line, q).wait_recv()
+            )
+        return act
+
+    def cross_planes(act):
+        for d in range(1, Z):
+            for line in (y, other_y):
+                for q in cross:
+                    from_planes(d, act(q, line))
+
+    for d in range(1, Z):
+        for n, q in enumerate(rest):
+            from_planes(d, pass_chunk(q))
+            if n == 0:
+                from_planes(d, pass_prow)
+        if d == FILL:
+            send_own(cross)
+            for q in cross:
+                chunk_copy(SIDE, y_row, q).wait_recv()
+                both(lambda way: chunk_copy(way, y_row, q).start())
+        if d == 1:
+            left_copy(c, x_peer, 0).wait_recv()
+            left_copy(core_peer, x_peer, 2).start()
+    cross_planes(pass_cross)
 
     def each_plane(act):
         for d in range(1, Z):
@@ -308,8 +321,7 @@
                     a = cols_smem[k // PB, c, t, 0, k % PB] // C
                     meta_ref[(i * C * KG + e) * KG + t] = (ranks >> (4 * a)) & 15
 
-    for d in range(2, Z):
-        pass_plane(d)
+    cross_planes(take_cross)
     for q in rest:
         chunk_copy(SIDE, y_row, q).wait_recv()
         each_plane(lambda plane: chunk_copy(SIDE, plane * NY + other_y, q).wait_recv())

time: 46.1 us -> 42.1 us (0.913)
  Pallas kernels: 45.3 us -> 41.3 us
    pallas_call x1, Pallas kernels: 41.5 us -> 37.5 us  [fast_on_device(): pl.pallas_call(functools.partial(gather_kernel, sizes), out_shape=(jax.Sh...]
where the time goes in v1:
time: 42.1 us; the launch traced here: 42 us
  Pallas kernels  41.3 us (98%)
  between operations  0.64 us (2%)
    pallas_call x1, Pallas kernels, fast_on_device(): pl.pallas_call(functools.partial(gather_kernel, sizes), out_shape=(jax.Sh...  37.5 us
    pallas_call x1, Pallas kernels, fast_on_device(): pl.pallas_call(functools.partial(square_kernel, sizes), out_shape=(pltpu....  3.8 us

profile of v1, /device:TPU:0, one launch (start us, length us, event | category | flops | bytes accessed | tf_op | source)
XLA Modules:
  0.0 42.0 jit_solution(9963666548190563520)
XLA Ops:
  0.6 37.5 %shard_map.49 = (bf16[8,12,128,128]{3,2,1,0:T(8,128)(2,1)S(1)}, bf16[4,12,128,128]{3,2,1,0:T(8,128)(2,1)S(1)}, s32[200]{0:T(256)S(1)}) custom-call(bf16[12,128,128]{2,1,0:T(8,128)(2,1)} %bitcast.5, s32[3,1,4]{2,1,0:T(1,128)} %bitcast.6), custom_call_target="tpu_custom_call" | custom-call | tf_op jit(solution)/shard_map/pallas_call | solution.py:430
  38.2 3.8 %shard_map.50 = (bf16[4,1,36,128,128]{4,3,2,1,0:T(8,128)(2,1)}, s32[4,1,36]{2,1,0:T(1,128)}, s32[1,4]{1,0:T(1,128)}) custom-call(s32[200]{0:T(256)S(1)} %get-tuple-element.9.meta_ref, bf16[4,12,128,128]{3,2,1,0:T(8,128)(2,1)S(1)} %get-tuple-element.10.left_ref, bf16[32,3,128,128]{3,2,1,0:T(8,128)(2,1)S(1)} %bitcast.4), custom_call_target="tpu_custom_call" | custom-call | tf_op jit(solution)/shard_map/pallas_call | solution.py:453
